TPU v7x, 32 devices: a whole 2x2x4 slice. The times are simulated.
32 devices in a mesh: dp: 4 (over y, core), vocab: 8 (over z, x).
Axes of the slice: x: 2, y: 2, z: 4, core: 2. Of those that a mesh axis runs over, the one named last changes fastest.
Arguments:
- hidden: bfloat16 [256, 3584], P('dp'), may hold values from -48 to 48
- embedding: bfloat16 [24576, 3584], P(('dp', 'vocab')), may hold values from -1 to 1
- targets: int32 [256], P('dp'), may hold values from 0 to 24575
- loss_weight: bfloat16 [256], P('dp'), may hold values from 1 to 10
Outputs:
- hidden_grad: bfloat16 [256, 3584], P('dp')
- table_grad: bfloat16 [24576, 3584], P(('dp', 'vocab'))
All inputs are finite; a program needn't handle non-finite values.
Results may differ from a plain program's by a relative error of at most 0.0049.
Values may be sent and summed in bfloat16 or wider, within the bound.
No kernel may reach another device: no remote copies, remote signals or barrier semaphores. Data moves between devices by JAX's collectives and lax.ppermute only.
A program may use at most 128 MiB of HBM per device.

v0:
```python
import jax
import jax.numpy as jnp
from jax import lax
from jax.sharding import PartitionSpec as P

soft_cap = 30.0
z_weight = 0.002


def body(hidden, embedding, targets, loss_weight):
    shard_rows = embedding.shape[0]
    group_hidden, group_weight = (
        lax.all_gather(hidden, "dp", axis=0, tiled=True),
        lax.all_gather(loss_weight, "dp", axis=0, tiled=True),
    )
    group_targets = lax.all_gather(targets, "dp", axis=0, tiled=True)
    logits = lax.dot_general(
        group_hidden, embedding, (((1,), (1,)), ((), ())), preferred_element_type=jnp.float32
    )
    capped = soft_cap * jnp.tanh(logits / soft_cap)
    exp_terms = jnp.exp(capped - soft_cap)
    partial_value = jnp.sum(exp_terms, axis=1)
    weight = group_weight.astype(jnp.float32)
    device_place = lax.axis_index("dp") * lax.axis_size("vocab") + lax.axis_index("vocab")
    exp_total = lax.psum(partial_value, ("dp", "vocab"))
    factor = weight * (1.0 + 2.0 * z_weight * (soft_cap + jnp.log(exp_total))) / exp_total
    columns = device_place * shard_rows + lax.iota(jnp.int32, shard_rows)
    target_hit = group_targets[:, None] == columns[None, :]
    softmax_part = factor[:, None] * exp_terms - jnp.where(target_hit, weight[:, None], 0.0)
    scores_grad = (softmax_part * (1.0 - (capped / soft_cap) ** 2)).astype(jnp.bfloat16)
    table_grad = lax.dot_general(
        scores_grad, group_hidden, (((0,), (0,)), ((), ())), preferred_element_type=jnp.float32
    ).astype(jnp.bfloat16)
    group_grad = lax.psum_scatter(
        jnp.dot(scores_grad, embedding, preferred_element_type=jnp.float32),
        "dp",
        scatter_dimension=0,
        tiled=True,
    )
    hidden_grad = lax.psum(group_grad, "vocab").astype(jnp.bfloat16)
    return (hidden_grad, table_grad)


def solution(mesh):
    return jax.shard_map(
        body,
        mesh=mesh,
        in_specs=(P("dp", None), P(("dp", "vocab"), None), P("dp"), P("dp")),
        out_specs=(P("dp", None), P(("dp", "vocab"), None)),
        check_vma=False,
    )
```

profile of v0, /device:TPU:0, one launch (start us, length us, event | category | flops | bytes accessed | tf_op | source)
XLA Modules:
  0.0 182.5 jit_solution(10813239611045289594)
XLA Ops:
  7.2 0.0 all-gather.2.cloned.1.call-start
  7.2 0.7 all-gather.2.cloned.1.call-update
  7.9 0.0 reduce-scatter.2.cloned.1.call-start
  8.0 1.2 dynamic-slice
  9.9 0.9 dynamic-update-slice
  10.7 8.4 %all-reduce = bf16[256]{0:T(256)(128)(2,1)S(1)} all-reduce(bf16[256]{0:T(256)(128)(2,1)S(1)} %dynamic-update-slice), channel_id=1, replica_groups=mesh['dp'=4,'vocab'=8] {'dp'}, use_global_device_ids=true, to_apply=%add | all-reduce | flops 256 | bytes 1024
  19.1 0.9 dynamic-update-slice.1
  20.0 4.5 %all-reduce.1 = s32[256]{0:T(256)S(1)} all-reduce(s32[256]{0:T(256)S(1)} %dynamic-update-slice.1), channel_id=1, replica_groups=mesh['dp'=4,'vocab'=8] {'dp'}, use_global_device_ids=true, to_apply=%add.1 | all-reduce | flops 256 | bytes 2048
  24.4 9.0 %all-gather.2.cloned.1.call-done = bf16[256,3584]{1,0:T(8,128)(2,1)} async-done(((bf16[64,3584]{1,0:T(8,128)(2,1)}), bf16[256,3584]{1,0:T(8,128)(2,1)}) %all-gather.2.cloned.1.call-update) | async-done | bytes 1835024 | tf_op jit(solution)/shard_map/all_gather | solution.py:13
  33.5 4.9 %fusion.1 = (f32[256]{0:T(256)S(1)}, f32[256,768]{1,0:T(8,128)S(1)}) fusion(bf16[256,3584]{1,0:T(8,128)(2,1)} %all-gather.2.cloned.1.call-done, bf16[768,3584]{1,0:T(8,128)(2,1)} %param.5), kind=kOutput, calls=%fused_computation.5 | convolution fusion | flops 1410072320 | bytes 8127488 | tf_op jit(solution)/shard_map/dot_general | solution.py:17
  38.4 39.3 %psum.14 = f32[256]{0:T(256)S(1)} all-reduce(f32[256]{0:T(256)S(1)} %get-tuple-element.2), channel_id=1, replica_groups=mesh['dp'=4,'vocab'=8] {'dp','vocab'}, use_global_device_ids=true, to_apply=%region_1.0 | all-reduce | flops 256 | bytes 2048 | tf_op jit(solution)/shard_map/psum | solution.py:25
  77.7 0.0 copy-start
  77.7 6.3 %fusion.2 = f32[256,3584]{1,0:T(8,128)} fusion(bf16[768,3584]{1,0:T(8,128)(2,1)} %param.5, f32[256,768]{1,0:T(8,128)S(1)} %get-tuple-element.3, f32[256]{0:T(256)S(1)} %convert_element_type.12, s32[768]{0:T(1024)S(1)} %iota_add_fusion, f32[256]{0:T(256)S(1)} %multiply_divide_fusion, s32[256]{0:T(256)S(1)} %all-reduce.1), kind=kOutput, calls=%fused_computation.8 | convolution fusion | flops 1411252224 | bytes 9967616 | tf_op jit(solution)/shard_map/dot_general | solution.py:35
  84.0 0.0 reduce-scatter.2.cloned.1.call-update
  84.0 0.0 copy-done
  84.0 4.3 %convolution_convert_fusion = bf16[768,3584]{1,0:T(8,128)(2,1)} fusion(bf16[256,3584]{1,0:T(8,128)(2,1)S(1)} %copy-done, f32[256,768]{1,0:T(8,128)S(1)} %get-tuple-element.3, f32[256]{0:T(256)S(1)} %convert_element_type.12, s32[768]{0:T(1024)S(1)} %iota_add_fusion, f32[256]{0:T(256)S(1)} %multiply_divide_fusion, s32[256]{0:T(256)S(1)} %all-reduce.1), kind=kOutput, calls=%fused_computation | convolution fusion | flops 1414004736 | bytes 8132608 | tf_op jit(solution)/shard_map/dot_general | solution.py:31
  88.3 37.9 %reduce-scatter.2.cloned.1.call-done = f32[64,3584]{1,0:T(8,128)} async-done(((f32[256,3584]{1,0:T(8,128)}), f32[64,3584]{1,0:T(8,128)}) %reduce-scatter.2.cloned.1.call-update) | async-done | bytes 917520 | tf_op jit(solution)/shard_map/reduce_scatter | solution.py:34
  126.2 49.4 %all-reduce.3 = bf16[64,3584]{1,0:T(8,128)(2,1)} all-reduce(f32[64,3584]{1,0:T(8,128)} %reduce-scatter.2.cloned.1.call-done), channel_id=1, replica_groups=mesh['dp'=4,'vocab'=8] {'vocab'}, use_global_device_ids=true, to_apply=%region_3.4 | all-reduce | flops 229376 | bytes 1376256 | tf_op jit(solution)/shard_map/psum | solution.py:40
  (5 shorter events, 0.0 us)
Async XLA Ops:
  7.2 26.3 %all-gather.2.cloned.1.call-start = ((), (), s32[]{:S(2)}) async-start(), calls=%async_computation.1 | async-start | bytes 2293760 | tf_op jit(solution)/shard_map/all_gather | solution.py:13
  7.9 118.3 %reduce-scatter.2.cloned.1.call-start = ((), (), s32[]{:S(2)}) async-start(), calls=%async_computation.2 | async-start | bytes 4587520 | tf_op jit(solution)/shard_map/reduce_scatter | solution.py:34
  77.7 6.3 %copy-start = (bf16[256,3584]{1,0:T(8,128)(2,1)S(1)}, bf16[256,3584]{1,0:T(8,128)(2,1)}, u32[]{:S(2)}) copy-start(bf16[256,3584]{1,0:T(8,128)(2,1)} %all-gather.2.cloned.1.call-done) | copy-start | bytes 5505028
Sparse Core Ops, SparseCore 0:
  9.5 23.9 all-gather.1
  84.1 42.0 reduce-scatter.1
where the time goes:
time: 183 us; the launch traced here: 182 us
  blocking collectives  102 us (56%)
  waiting for transfers between devices  47.6 us (26%)
  matrix products  15.4 us (8%)
  between operations  14.7 us (8%)
  local copies, waits for them, and re-layouts  2.97 us (2%)
    psum x1, blocking collectives, body(): hidden_grad = lax.psum(group_grad, 'vocab').astype(jnp.bfloat16)  49.4 us
    psum x1, blocking collectives, body(): exp_total = lax.psum(partial_value, ('dp', 'vocab'))  39.3 us
    reduce_scatter x1, waiting for transfers between devices, body(): lax.psum_scatter(jnp.dot(scores_grad, embedding, preferred_element_type=j...  37.9 us
    unnamed x2, blocking collectives  12.8 us
    all_gather x1, waiting for transfers between devices, body(): lax.all_gather(hidden, 'dp', axis=0, tiled=True)  9.04 us
    dot_general x1, matrix products, body(): jnp.dot(scores_grad, embedding, preferred_element_type=jnp.float32)  6.28 us
    dot_general x1, matrix products, body(): lax.dot_general(group_hidden, embedding, (((1,), (1,)), ((), ())), prefer...  4.91 us
    dot_general x1, matrix products, body(): lax.dot_general(scores_grad, group_hidden, (((0,), (0,)), ((), ())), pref...  4.26 us
  transfers between devices with their start and end apart: 2, of which 2 were waited for; matrix products, arithmetic and copies ran while one was open for 4% of the time, Pallas kernels for 0%

commit v1 on v0

v1 whole, which is shorter than its diff:
```python
import jax
import jax.numpy as jnp
from jax import lax
from jax.sharding import PartitionSpec as P

soft_cap = 30.0
z_weight = 0.002
bf16 = jnp.bfloat16
f32 = jnp.float32


def exchange(x, axis, bit):
    return lax.ppermute(x, axis, [(i, i ^ bit) for i in range(lax.axis_size(axis))])


def axis_bits(axis):
    size = lax.axis_size(axis)
    assert size & (size - 1) == 0
    return [1 << b for b in range(size.bit_length() - 1)]


def gather_relative(x):
    for bit in reversed(axis_bits("dp")):
        x = jnp.concatenate([x, exchange(x, "dp", bit)], axis=0)
    return x


def relative_to_absolute(x, inverse=False):
    size = lax.axis_size("dp")
    nbits = size.bit_length() - 1
    place = lax.axis_index("dp")
    x = x.reshape((2,) * nbits + (-1,))
    def flip(x):
        for b in range(nbits):
            hit = ((place >> b) & 1) == 1
            x = jnp.where(hit, lax.rev(x, (b,)), x)
        return x
    order = tuple(reversed(range(nbits))) + (nbits,)
    if inverse:
        return flip(x.transpose(order)).reshape(-1)
    return flip(x).transpose(order).reshape(-1)


def scatter_relative(x):
    for bit in axis_bits("dp"):
        half = x.shape[0] // 2
        other = exchange(x[half:].astype(bf16), "dp", bit)
        x = x[:half].astype(f32) + other.astype(f32)
    return x.astype(bf16)


def sum_over_vocab(x):
    size = lax.axis_size("vocab")
    rows = x.shape[0] // size
    parts = lax.all_to_all(x.reshape(size, rows, x.shape[1]), "vocab", 0, 0)
    total = jnp.sum(parts.astype(f32), axis=0).astype(bf16)
    spread = jnp.broadcast_to(total[None], (size,) + total.shape)
    return lax.all_to_all(spread, "vocab", 0, 0).reshape(x.shape)


def body(hidden, embedding, targets, loss_weight):
    shard_rows = embedding.shape[0]
    both = ("dp", "vocab")
    n_all = lax.axis_size("dp") * lax.axis_size("vocab")
    group_hidden = gather_relative(hidden)
    side = gather_relative(jnp.stack([loss_weight.astype(f32), targets.astype(f32)], axis=1))
    weight = side[:, :1]
    group_targets = side[:, 1:].astype(jnp.int32)
    logits = lax.dot_general(
        group_hidden, embedding, (((1,), (1,)), ((), ())), preferred_element_type=f32
    )
    capped = soft_cap * jnp.tanh(logits / soft_cap)
    exp_terms = jnp.exp(capped - soft_cap)
    partial_value = relative_to_absolute(jnp.sum(exp_terms, axis=1))
    spread = jnp.broadcast_to(partial_value[None], (n_all,) + partial_value.shape)
    exp_total = jnp.sum(lax.all_to_all(spread, both, 0, 0), axis=0)
    exp_total = relative_to_absolute(exp_total, inverse=True)[:, None]
    factor = weight * (1.0 + 2.0 * z_weight * (soft_cap + jnp.log(exp_total))) / exp_total
    columns = lax.axis_index(both) * shard_rows + lax.iota(jnp.int32, shard_rows)
    target_hit = group_targets == columns[None, :]
    softmax_part = factor * exp_terms - jnp.where(target_hit, weight, 0.0)
    scores_grad = (softmax_part * (1.0 - (capped / soft_cap) ** 2)).astype(bf16)
    group_grad = jnp.dot(scores_grad, embedding, preferred_element_type=f32)
    hidden_grad = sum_over_vocab(scatter_relative(group_grad))
    table_grad = lax.dot_general(
        scores_grad, group_hidden, (((0,), (0,)), ((), ())), preferred_element_type=f32
    ).astype(bf16)
    return (hidden_grad, table_grad)


def solution(mesh):
    return jax.shard_map(
        body,
        mesh=mesh,
        in_specs=(P("dp", None), P(("dp", "vocab"), None), P("dp"), P("dp")),
        out_specs=(P("dp", None), P(("dp", "vocab"), None)),
        check_vma=False,
    )
```

time: 183 us -> 93 us (0.51)
  blocking collectives: 102 us -> 15.4 us
  starting transfers between devices: 0.08 us -> 14.1 us
  between operations: 14.7 us -> 0.76 us
  waiting for transfers between devices: 47.6 us -> 41.3 us
  other arithmetic: 0.02 us -> 3.97 us
  matrix products: 15.4 us -> 12.9 us
    psum x2 -> x0, blocking collectives: 88.7 us -> none  [the longest x1 49.4 us: body(): hidden_grad = lax.psum(group_grad, 'vocab').astype(jnp.bfloat16)]
    reduce_scatter x1 -> x0, waiting for transfers between devices: 37.9 us -> none  [body(): lax.psum_scatter(jnp.dot(scores_grad, embedding, preferred_element_type=j...]
    ppermute x0 -> x6, waiting for transfers between devices: none -> 25.7 us  [exchange(): lax.ppermute(x, axis, [(i, i ^ bit) for i in range(lax.axis_size(axis))])]
    all_to_all x0 -> x2, waiting for transfers between devices: none -> 15.6 us  [the longest x1 8.5 us: sum_over_vocab(): return lax.all_to_all(spread, 'vocab', 0, 0).reshape(x.shape)]
    all_to_all x0 -> x1, blocking collectives: none -> 15.4 us  [sum_over_vocab(): parts = lax.all_to_all(x.reshape(size, rows, x.shape[1]), 'vocab', 0, 0)]
    unnamed x2 -> x0, blocking collectives: 12.8 us -> none
    all_to_all x0 -> x2, starting transfers between devices: none -> 9.54 us  [the longest x1 6.07 us: body(): exp_total = jnp.sum(lax.all_to_all(spread, both, 0, 0), axis=0)]
    all_gather x1 -> x0, waiting for transfers between devices: 9.04 us -> none  [body(): lax.all_gather(hidden, 'dp', axis=0, tiled=True)]
  transfers between devices with their start and end apart: 2 -> 8, of which waited for: 2 -> 6; matrix products, arithmetic and copies ran while one was open for 4% -> 15% of each run, Pallas kernels for 0% -> 0%
where the time goes in v1:
time: 93 us; the launch traced here: 92.5 us
  waiting for transfers between devices  41.3 us (44%)
  blocking collectives  15.4 us (17%)
  starting transfers between devices  14.1 us (15%)
  matrix products  12.9 us (14%)
  local copies, waits for them, and re-layouts  4.06 us (4%)
  other arithmetic  3.97 us (4%)
    ppermute x6, waiting for transfers between devices, exchange(): lax.ppermute(x, axis, [(i, i ^ bit) for i in range(lax.axis_size(axis))])  25.7 us
    all_to_all x1, blocking collectives, sum_over_vocab(): parts = lax.all_to_all(x.reshape(size, rows, x.shape[1]), 'vocab', 0, 0)  15.4 us
    all_to_all x1, waiting for transfers between devices, sum_over_vocab(): return lax.all_to_all(spread, 'vocab', 0, 0).reshape(x.shape)  8.5 us
    all_to_all x1, waiting for transfers between devices, body(): exp_total = jnp.sum(lax.all_to_all(spread, both, 0, 0), axis=0)  7.1 us
    all_to_all x1, starting transfers between devices, body(): exp_total = jnp.sum(lax.all_to_all(spread, both, 0, 0), axis=0)  6.07 us
    ppermute x6, starting transfers between devices, exchange(): lax.ppermute(x, axis, [(i, i ^ bit) for i in range(lax.axis_size(axis))])  4.58 us
    dot_general x1, matrix products, body(): group_grad = jnp.dot(scores_grad, embedding, preferred_element_type=f32)  4.35 us
    dot_general x1, matrix products, body(): lax.dot_general(group_hidden, embedding, (((1,), (1,)), ((), ())), prefer...  4.35 us
  transfers between devices with their start and end apart: 8, of which 6 were waited for; matrix products, arithmetic and copies ran while one was open for 15% of the time, Pallas kernels for 0%

profile of v1, /device:TPU:0, one launch (start us, length us, event | category | flops | bytes accessed | tf_op | source)
XLA Modules:
  0.0 92.5 jit_solution(9154353906497450406)
XLA Ops:
  0.6 3.1 %collective-permute-start.2 = (bf16[64,3584]{1,0:T(8,128)(2,1)}, bf16[64,3584]{1,0:T(8,128)(2,1)S(1)}, u32[]{:S(2)}, u32[]{:S(2)}) collective-permute-start(bf16[64,3584]{1,0:T(8,128)(2,1)} %param.4), channel_id=1, source_target_pairs={{0,16},{8,24},{16,0},{24,8},{1,17},{9,25},{17,1},{25,9},{2,18},{10... | collective-permute-start | bytes 1376264 | tf_op jit(solution)/shard_map/ppermute | solution.py:13
  3.7 0.7 convert_bitcast_fusion
  4.4 0.7 bitcast_convert_fusion
  5.2 9.3 %collective-permute-done.2 = bf16[64,3584]{1,0:T(8,128)(2,1)S(1)} collective-permute-done((bf16[64,3584]{1,0:T(8,128)(2,1)}, bf16[64,3584]{1,0:T(8,128)(2,1)S(1)}, u32[]{:S(2)}, u32[]{:S(2)}) %collective-permute-start.2) | collective-permute-done | bytes 458784 | tf_op jit(solution)/shard_map/ppermute | solution.py:13
  14.4 2.0 %pad_maximum_fusion = bf16[128,3584]{1,0:T(8,128)(2,1)} fusion(bf16[64,3584]{1,0:T(8,128)(2,1)S(1)} %collective-permute-done.2, bf16[64,3584]{1,0:T(8,128)(2,1)} %param.4), kind=kLoop, calls=%fused_computation.8 | loop fusion | flops 1835008 | bytes 1835008 | tf_op jit(solution)/shard_map/concatenate | solution.py:24
  16.6 0.5 collective-permute-start.1
  17.1 2.1 %collective-permute-done.3 = bf16[128,3584]{1,0:T(8,128)(2,1)} collective-permute-done((bf16[128,3584]{1,0:T(8,128)(2,1)}, bf16[128,3584]{1,0:T(8,128)(2,1)}, u32[]{:S(2)}, u32[]{:S(2)}) %collective-permute-start.3) | collective-permute-done | bytes 917536 | tf_op jit(solution)/shard_map/ppermute | solution.py:13
  19.3 1.2 %constant_dynamic-update-slice_fusion = bf16[256,3584]{1,0:T(8,128)(2,1)S(1)} fusion(bf16[256,3584]{1,0:T(8,128)(2,1)S(1)} %constant_dynamic-update-slice_fusion.1, bf16[128,3584]{1,0:T(8,128)(2,1)} %collective-permute-done.3), kind=kLoop, calls=%fused_computation.13 | loop fusion | bytes 1835008 | tf_op jit(solution)/shard_map/concatenate | solution.py:24
  20.5 4.3 %fusion.2 = (f32[256]{0:T(256)S(1)}, f32[256,768]{1,0:T(8,128)S(1)}) fusion(bf16[256,3584]{1,0:T(8,128)(2,1)S(1)} %constant_dynamic-update-slice_fusion, bf16[768,3584]{1,0:T(8,128)(2,1)} %param.5), kind=kOutput, calls=%fused_computation.11 | convolution fusion | flops 1410072320 | bytes 8127488 | tf_op jit(solution)/shard_map/dot_general | solution.py:69
  25.1 0.6 broadcast_in_dim.29
  25.7 6.1 %all-to-all-start = ((f32[32,1,256]{2,1,0:T(1,128)}), f32[32,1,256]{2,1,0:T(1,128)S(1)}, u32[]{:S(2)}, u32[]{:S(2)}) async-start(f32[32,1,256]{2,1,0:T(1,128)} %broadcast_in_dim.29), calls=%async_computation | async-start | bytes 65536 | tf_op jit(solution)/shard_map/all_to_all | solution.py:76
  31.9 7.1 %all-to-all-done = f32[32,1,256]{2,1,0:T(1,128)S(1)} async-done(((f32[32,1,256]{2,1,0:T(1,128)}), f32[32,1,256]{2,1,0:T(1,128)S(1)}, u32[]{:S(2)}, u32[]{:S(2)}) %all-to-all-start) | async-done | bytes 32800 | tf_op jit(solution)/shard_map/all_to_all | solution.py:76
  39.3 4.3 %fusion.4 = f32[256,3584]{1,0:T(8,128)S(1)} fusion(bf16[768,3584]{1,0:T(8,128)(2,1)} %param.5, f32[256,768]{1,0:T(8,128)S(1)} %get-tuple-element.6, f32[256]{0:T(256)S(1)} %bitcast.27, s32[768]{0:T(1024)S(1)} %iota_add_fusion, f32[256]{0:T(256)S(1)} %bitcast.25, s32[256]{0:T(256)S(1)} %bitcast.23), kind=kOutput, calls=%fused_computation.29 | convolution fusion | flops 1411252224 | bytes 9967616 | tf_op jit(solution)/shard_map/dot_general | solution.py:83
  43.7 0.2 collective-permute-start.4
  43.9 2.4 %collective-permute-done.4 = bf16[128,3584]{1,0:T(8,128)(2,1)S(1)} collective-permute-done((bf16[128,3584]{1,0:T(8,128)(2,1)S(1)}, bf16[128,3584]{1,0:T(8,128)(2,1)S(1)}, u32[]{:S(2)}, u32[]{:S(2)}) %collective-permute-start.4) | collective-permute-done | bytes 917536 | tf_op jit(solution)/shard_map/ppermute | solution.py:13
  46.3 0.2 slice_add_fusion
  46.6 0.7 collective-permute-start.5
  47.2 11.9 %collective-permute-done.5 = bf16[64,3584]{1,0:T(8,128)(2,1)S(1)} collective-permute-done((bf16[64,3584]{1,0:T(8,128)(2,1)S(1)}, bf16[64,3584]{1,0:T(8,128)(2,1)S(1)}, u32[]{:S(2)}, u32[]{:S(2)}) %collective-permute-start.5) | collective-permute-done | bytes 458784 | tf_op jit(solution)/shard_map/ppermute | solution.py:13
  59.3 15.4 %all_to_all.16 = bf16[8,8,3584]{2,1,0:T(8,128)(2,1)S(1)} all-to-all(bf16[8,8,3584]{2,1,0:T(8,128)(2,1)S(1)} %fusion.3), channel_id=1, replica_groups=mesh['dp'=4,'vocab'=8] {'vocab'}, dimensions={0} | all-to-all | bytes 917504 | tf_op jit(solution)/shard_map/all_to_all | solution.py:55
  74.7 0.8 broadcast_in_dim.33
  75.5 3.5 %all-to-all-start.2 = ((bf16[8,8,3584]{2,1,0:T(8,128)(2,1)}), bf16[8,8,3584]{2,1,0:T(8,128)(2,1)S(1)}, u32[]{:S(2)}, u32[]{:S(2)}) async-start(bf16[8,8,3584]{2,1,0:T(8,128)(2,1)} %broadcast_in_dim.33), calls=%async_computation.2 | async-start | bytes 917504 | tf_op jit(solution)/shard_map/all_to_all | solution.py:58
  79.0 4.3 %convolution_convert_fusion = bf16[768,3584]{1,0:T(8,128)(2,1)} fusion(bf16[256,3584]{1,0:T(8,128)(2,1)S(1)} %constant_dynamic-update-slice_fusion, f32[256,768]{1,0:T(8,128)S(1)} %get-tuple-element.6, f32[256]{0:T(256)S(1)} %bitcast.28, s32[768]{0:T(1024)S(1)} %iota_add_fusion, f32[256]{0:T(256)S(1)} %bitcast.26, s32[256]{0:T(256)S(1)} %bitcast.24), kind=kOutput, calls=%fused_computation | convolution fusion | flops 1414004736 | bytes 8132608 | tf_op jit(solution)/shard_map/dot_general | solution.py:85
  83.3 8.5 %all-to-all-done.2 = bf16[8,8,3584]{2,1,0:T(8,128)(2,1)S(1)} async-done(((bf16[8,8,3584]{2,1,0:T(8,128)(2,1)}), bf16[8,8,3584]{2,1,0:T(8,128)(2,1)S(1)}, u32[]{:S(2)}, u32[]{:S(2)}) %all-to-all-start.2) | async-done | bytes 458784 | tf_op jit(solution)/shard_map/all_to_all | solution.py:58
  91.8 0.8 copy.20
  (30 shorter events, 1.2 us)
Async XLA Ops:
  0.6 15.8 %copy-start = (bf16[64,3584]{1,0:T(8,128)(2,1)S(1)}, bf16[64,3584]{1,0:T(8,128)(2,1)}, u32[]{:S(2)}) copy-start(bf16[64,3584]{1,0:T(8,128)(2,1)} %param.4) | copy-start | bytes 1376260
  0.6 13.8 %collective-permute-start.2 = (bf16[64,3584]{1,0:T(8,128)(2,1)}, bf16[64,3584]{1,0:T(8,128)(2,1)S(1)}, u32[]{:S(2)}, u32[]{:S(2)}) collective-permute-start(bf16[64,3584]{1,0:T(8,128)(2,1)} %param.4), channel_id=1, source_target_pairs={{0,16},{8,24},{16,0},{24,8},{1,17},{9,25},{17,1},{25,9},{2,18},{10... | collective-permute-start | bytes 1376264 | tf_op jit(solution)/shard_map/ppermute | solution.py:13
  5.0 11.5 %collective-permute-start = (f32[64,2]{0,1:T(2,128)S(1)}, f32[64,2]{0,1:T(2,128)S(1)}, u32[]{:S(2)}, u32[]{:S(2)}) collective-permute-start(f32[64,2]{0,1:T(2,128)S(1)} %pad_maximum_fusion.2), channel_id=1, source_target_pairs={{0,16},{8,24},{16,0},{24,8},{1,17},{9,25},{17,1},{25,9},{2,18},{10... | collective-permute-start | bytes 1544 | tf_op jit(solution)/shard_map/ppermute | solution.py:13
  16.4 2.8 %collective-permute-start.3 = (bf16[128,3584]{1,0:T(8,128)(2,1)}, bf16[128,3584]{1,0:T(8,128)(2,1)}, u32[]{:S(2)}, u32[]{:S(2)}) collective-permute-start(bf16[128,3584]{1,0:T(8,128)(2,1)} %pad_maximum_fusion), channel_id=1, source_target_pairs={{0,8},{8,0},{16,24},{24,16},{1,9},{9,1},{17,25},{25,17},{2,10},{10... | collective-permute-start | bytes 2752520 | tf_op jit(solution)/shard_map/ppermute | solution.py:13
  16.6 15.2 %collective-permute-start.1 = (f32[128,2]{0,1:T(2,128)S(1)}, f32[128,2]{0,1:T(2,128)S(1)}, u32[]{:S(2)}, u32[]{:S(2)}) collective-permute-start(f32[128,2]{0,1:T(2,128)S(1)} %pad_maximum_fusion.3), channel_id=1, source_target_pairs={{0,8},{8,0},{16,24},{24,16},{1,9},{9,1},{17,25},{25,17},{2,10},{10... | collective-permute-start | bytes 3080 | tf_op jit(solution)/shard_map/ppermute | solution.py:13
  25.7 13.3 %all-to-all-start = ((f32[32,1,256]{2,1,0:T(1,128)}), f32[32,1,256]{2,1,0:T(1,128)S(1)}, u32[]{:S(2)}, u32[]{:S(2)}) async-start(f32[32,1,256]{2,1,0:T(1,128)} %broadcast_in_dim.29), calls=%async_computation | async-start | bytes 65536 | tf_op jit(solution)/shard_map/all_to_all | solution.py:76
  43.7 2.5 %collective-permute-start.4 = (bf16[128,3584]{1,0:T(8,128)(2,1)S(1)}, bf16[128,3584]{1,0:T(8,128)(2,1)S(1)}, u32[]{:S(2)}, u32[]{:S(2)}) collective-permute-start(bf16[128,3584]{1,0:T(8,128)(2,1)S(1)} %slice.42), channel_id=1, source_target_pairs={{0,8},{8,0},{16,24},{24,16},{1,9},{9,1},{17,25},{25,17},{2,10},{10... | collective-permute-start | bytes 2752520 | tf_op jit(solution)/shard_map/ppermute | solution.py:13
  46.6 12.6 %collective-permute-start.5 = (bf16[64,3584]{1,0:T(8,128)(2,1)S(1)}, bf16[64,3584]{1,0:T(8,128)(2,1)S(1)}, u32[]{:S(2)}, u32[]{:S(2)}) collective-permute-start(bf16[64,3584]{1,0:T(8,128)(2,1)S(1)} %slice.43), channel_id=1, source_target_pairs={{0,16},{8,24},{16,0},{24,8},{1,17},{9,25},{17,1},{25,9},{2,18},{10... | collective-permute-start | bytes 1376264 | tf_op jit(solution)/shard_map/ppermute | solution.py:13
  75.5 16.2 %all-to-all-start.2 = ((bf16[8,8,3584]{2,1,0:T(8,128)(2,1)}), bf16[8,8,3584]{2,1,0:T(8,128)(2,1)S(1)}, u32[]{:S(2)}, u32[]{:S(2)}) async-start(bf16[8,8,3584]{2,1,0:T(8,128)(2,1)} %broadcast_in_dim.33), calls=%async_computation.2 | async-start | bytes 917504 | tf_op jit(solution)/shard_map/all_to_all | solution.py:58

commit v2 on v1

--- a/solution.py
+++ b/solution.py
@@ -20,9 +20,11 @@
 
 
 def gather_relative(x):
-    for bit in reversed(axis_bits("dp")):
-        x = jnp.concatenate([x, exchange(x, "dp", bit)], axis=0)
-    return x
+    near, *far = axis_bits("dp")
+    pieces = [x]
+    for bit in reversed(far):
+        pieces = pieces + [exchange(p, "dp", bit) for p in pieces]
+    return jnp.concatenate(pieces + [exchange(p, "dp", near) for p in pieces], axis=0)
 
 
 def relative_to_absolute(x, inverse=False):
@@ -41,21 +43,57 @@
     return flip(x).transpose(order).reshape(-1)
 
 
-def scatter_relative(x):
-    for bit in axis_bits("dp"):
-        half = x.shape[0] // 2
-        other = exchange(x[half:].astype(bf16), "dp", bit)
-        x = x[:half].astype(f32) + other.astype(f32)
-    return x.astype(bf16)
+def take(x, index, rows, axis=0):
+    return lax.dynamic_slice_in_dim(x, index * rows, rows, axis)
 
 
-def sum_over_vocab(x):
+def halve(x, bit):
+    half = x.shape[0] // 2
+    other = exchange(x[half:].astype(bf16), "dp", bit)
+    return x[:half].astype(f32) + other.astype(f32)
+
+
+def halve_vocab(x, blocks):
+    place = lax.axis_index("vocab") % 2
+    half = x.shape[0] // (2 * blocks)
+    x = x.reshape(blocks, 2 * half, x.shape[1])
+    other = exchange(take(x, 1 - place, half, 1).astype(bf16), "vocab", 1)
+    return (take(x, place, half, 1).astype(f32) + other.astype(f32)).reshape(blocks * half, -1)
+
+
+def shift_pairs(x, k):
     size = lax.axis_size("vocab")
-    rows = x.shape[0] // size
-    parts = lax.all_to_all(x.reshape(size, rows, x.shape[1]), "vocab", 0, 0)
-    total = jnp.sum(parts.astype(f32), axis=0).astype(bf16)
-    spread = jnp.broadcast_to(total[None], (size,) + total.shape)
-    return lax.all_to_all(spread, "vocab", 0, 0).reshape(x.shape)
+    return lax.ppermute(x, "vocab", [(i, (i + 2 * k) % size) for i in range(size)])
+
+
+def hops(count):
+    return sorted(range(1, count), key=lambda k: -min(k, count - k))
+
+
+def reduce_hidden(left, right):
+    near, *far = axis_bits("dp")
+    left, right = halve(left, near), halve(right, near)
+    blocks = lax.axis_size("dp") // 2
+    right = halve_vocab(right, blocks)
+    for bit in far:
+        left = halve(left, bit)
+        right = halve(right, bit)
+    left = halve_vocab(left, 1)
+    part = jnp.concatenate([left, right], axis=1)
+    count = lax.axis_size("vocab") // 2
+    place = lax.axis_index("vocab") // 2
+    rows = part.shape[0] // count
+    total = take(part, place, rows)
+    sent = part.astype(bf16)
+    for k in hops(count):
+        total = total + shift_pairs(take(sent, (place + k) % count, rows), k).astype(f32)
+    total = total.astype(bf16)
+    out = jnp.zeros(part.shape, bf16)
+    for k, piece in [(0, total)] + [(k, shift_pairs(total, k)) for k in hops(count)]:
+        out = lax.dynamic_update_slice_in_dim(out, piece, ((place - k) % count) * rows, 0)
+    other = exchange(out, "vocab", 1)
+    low = lax.axis_index("vocab") % 2 == 0
+    return jnp.where(low, jnp.concatenate([out, other], 0), jnp.concatenate([other, out], 0))
 
 
 def body(hidden, embedding, targets, loss_weight):
@@ -73,15 +111,17 @@
     exp_terms = jnp.exp(capped - soft_cap)
     partial_value = relative_to_absolute(jnp.sum(exp_terms, axis=1))
     spread = jnp.broadcast_to(partial_value[None], (n_all,) + partial_value.shape)
-    exp_total = jnp.sum(lax.all_to_all(spread, both, 0, 0), axis=0)
-    exp_total = relative_to_absolute(exp_total, inverse=True)[:, None]
+    totals = lax.all_to_all(spread, both, 0, 0)
+    columns = lax.axis_index(both) * shard_rows + lax.iota(jnp.int32, shard_rows)
+    hit_weight = jnp.where(group_targets == columns[None, :], weight, 0.0)
+    slope = 1.0 - (capped / soft_cap) ** 2
+    exp_total = relative_to_absolute(jnp.sum(totals, axis=0), inverse=True)[:, None]
     factor = weight * (1.0 + 2.0 * z_weight * (soft_cap + jnp.log(exp_total))) / exp_total
-    columns = lax.axis_index(both) * shard_rows + lax.iota(jnp.int32, shard_rows)
-    target_hit = group_targets == columns[None, :]
-    softmax_part = factor * exp_terms - jnp.where(target_hit, weight, 0.0)
-    scores_grad = (softmax_part * (1.0 - (capped / soft_cap) ** 2)).astype(bf16)
-    group_grad = jnp.dot(scores_grad, embedding, preferred_element_type=f32)
-    hidden_grad = sum_over_vocab(scatter_relative(group_grad))
+    scores_grad = ((factor * exp_terms - hit_weight) * slope).astype(bf16)
+    cut = embedding.shape[1] // 2
+    left = jnp.dot(scores_grad, embedding[:, :cut], preferred_element_type=f32)
+    right = jnp.dot(scores_grad, embedding[:, cut:], preferred_element_type=f32)
+    hidden_grad = reduce_hidden(left, right)
     table_grad = lax.dot_general(
         scores_grad, group_hidden, (((0,), (0,)), ((), ())), preferred_element_type=f32
     ).astype(bf16)

time: 93 us -> 82.6 us (0.89)
  blocking collectives: 15.4 us -> 0 us
  starting transfers between devices: 14.1 us -> 19.5 us
  matrix products: 12.9 us -> 14.5 us
  other arithmetic: 3.97 us -> 2.72 us
    all_to_all x1 -> x0, blocking collectives: 15.4 us -> none  [sum_over_vocab(): parts = lax.all_to_all(x.reshape(size, rows, x.shape[1]), 'vocab', 0, 0)]
    ppermute x0 -> x6, waiting for transfers between devices: none -> 8.57 us  [shift_pairs(): lax.ppermute(x, 'vocab', [(i, (i + 2 * k) % size) for i in range(size)])]
    all_to_all x2 -> x1, waiting for transfers between devices: 15.6 us -> 7.09 us  [body(): totals = lax.all_to_all(spread, both, 0, 0)]
    ppermute x0 -> x6, starting transfers between devices: none -> 6.87 us  [shift_pairs(): lax.ppermute(x, 'vocab', [(i, (i + 2 * k) % size) for i in range(size)])]
    all_to_all x2 -> x1, starting transfers between devices: 9.54 us -> 4.89 us  [body(): totals = lax.all_to_all(spread, both, 0, 0)]
    ppermute x6 -> x13, starting transfers between devices: 4.58 us -> 7.75 us  [exchange(): lax.ppermute(x, axis, [(i, i ^ bit) for i in range(lax.axis_size(axis))])]
    concatenate x3 -> x1, other arithmetic: 2.15 us -> 0.08 us  [gather_relative(): jnp.concatenate(pieces + [exchange(p, 'dp', near) for p in pieces], axis=0)]
    dot_general x1 -> x2, matrix products: 4.35 us -> 5.9 us  [the longest x1 3.02 us: body(): left = jnp.dot(scores_grad, embedding[:, :cut], preferred_element_type=f32)]
  transfers between devices with their start and end apart: 8 -> 20, of which waited for: 6 -> 15; matrix products, arithmetic and copies ran while one was open for 15% -> 17% of each run, Pallas kernels for 0% -> 0%
where the time goes in v2:
time: 82.6 us; the launch traced here: 82.3 us
  waiting for transfers between devices  41 us (50%)
  starting transfers between devices  19.5 us (24%)
  matrix products  14.5 us (18%)
  local copies, waits for them, and re-layouts  3.67 us (4%)
  other arithmetic  2.72 us (3%)
  between operations  0.92 us (1%)
    ppermute x13, waiting for transfers between devices, exchange(): lax.ppermute(x, axis, [(i, i ^ bit) for i in range(lax.axis_size(axis))])  25.3 us
    ppermute x6, waiting for transfers between devices, shift_pairs(): lax.ppermute(x, 'vocab', [(i, (i + 2 * k) % size) for i in range(size)])  8.57 us
    ppermute x13, starting transfers between devices, exchange(): lax.ppermute(x, axis, [(i, i ^ bit) for i in range(lax.axis_size(axis))])  7.75 us
    all_to_all x1, waiting for transfers between devices, body(): totals = lax.all_to_all(spread, both, 0, 0)  7.09 us
    ppermute x6, starting transfers between devices, shift_pairs(): lax.ppermute(x, 'vocab', [(i, (i + 2 * k) % size) for i in range(size)])  6.87 us
    all_to_all x1, starting transfers between devices, body(): totals = lax.all_to_all(spread, both, 0, 0)  4.89 us
    dot_general x1, matrix products, body(): lax.dot_general(group_hidden, embedding, (((1,), (1,)), ((), ())), prefer...  4.34 us
    dot_general x1, matrix products, body(): lax.dot_general(scores_grad, group_hidden, (((0,), (0,)), ((), ())), pref...  4.25 us
  transfers between devices with their start and end apart: 20, of which 15 were waited for; matrix products, arithmetic and copies ran while one was open for 17% of the time, Pallas kernels for 0%

profile of v2, /device:TPU:0, one launch (start us, length us, event | category | flops | bytes accessed | tf_op | source)
XLA Modules:
  0.0 82.3 jit_solution(12581644058281183041)
XLA Ops:
  2.5 2.6 %collective-permute-start = (f32[64,2]{0,1:T(2,128)S(1)}, f32[64,2]{0,1:T(2,128)S(1)}, u32[]{:S(2)}, u32[]{:S(2)}) collective-permute-start(f32[64,2]{0,1:T(2,128)S(1)} %pad_maximum_fusion.2), channel_id=1, source_target_pairs={{0,16},{8,24},{16,0},{24,8},{1,17},{9,25},{17,1},{25,9},{2,18},{10... | collective-permute-start | bytes 1544 | tf_op jit(solution)/shard_map/ppermute | solution.py:13
  5.3 1.0 %constant_dynamic-update-slice_fusion.3 = bf16[256,3584]{1,0:T(8,128)(2,1)S(1)} fusion(bf16[64,3584]{1,0:T(8,128)(2,1)} %param.4), kind=kLoop, calls=%fused_computation.39 | loop fusion | bytes 917504
  6.8 11.0 %collective-permute-done.3 = bf16[64,3584]{1,0:T(8,128)(2,1)S(1)} collective-permute-done((bf16[64,3584]{1,0:T(8,128)(2,1)}, bf16[64,3584]{1,0:T(8,128)(2,1)S(1)}, u32[]{:S(2)}, u32[]{:S(2)}) %collective-permute-start.3) | collective-permute-done | bytes 458784 | tf_op jit(solution)/shard_map/ppermute | solution.py:13
  18.0 1.7 %collective-permute-done.5 = bf16[64,3584]{1,0:T(8,128)(2,1)S(1)} collective-permute-done((bf16[64,3584]{1,0:T(8,128)(2,1)S(1)}, bf16[64,3584]{1,0:T(8,128)(2,1)S(1)}, u32[]{:S(2)}, u32[]{:S(2)}) %collective-permute-start.5) | collective-permute-done | bytes 458784 | tf_op jit(solution)/shard_map/ppermute | solution.py:13
  19.7 4.3 %fusion.5 = (f32[256]{0:T(256)S(1)}, f32[256,768]{1,0:T(8,128)S(1)}) fusion(bf16[256,3584]{1,0:T(8,128)(2,1)S(1)} %constant_dynamic-update-slice_fusion, bf16[768,3584]{1,0:T(8,128)(2,1)} %param.5), kind=kOutput, calls=%fused_computation.13 | convolution fusion | flops 1410072320 | bytes 8127488 | tf_op jit(solution)/shard_map/dot_general | solution.py:107
  24.9 4.9 %all-to-all-start = ((f32[32,1,256]{2,1,0:T(1,128)}), f32[32,1,256]{2,1,0:T(1,128)S(1)}, u32[]{:S(2)}, u32[]{:S(2)}) async-start(f32[32,1,256]{2,1,0:T(1,128)} %broadcast_in_dim.27), calls=%async_computation | async-start | bytes 65536 | tf_op jit(solution)/shard_map/all_to_all | solution.py:114
  29.9 7.1 %all-to-all-done = f32[32,1,256]{2,1,0:T(1,128)S(1)} async-done(((f32[32,1,256]{2,1,0:T(1,128)}), f32[32,1,256]{2,1,0:T(1,128)S(1)}, u32[]{:S(2)}, u32[]{:S(2)}) %all-to-all-start) | async-done | bytes 32800 | tf_op jit(solution)/shard_map/all_to_all | solution.py:114
  37.3 2.9 %fusion = f32[256,1792]{1,0:T(8,128)S(1)} fusion(bf16[768,3584]{1,0:T(8,128)(2,1)} %param.5, f32[256,768]{1,0:T(8,128)S(1)} %get-tuple-element.11, f32[256]{0:T(256)S(1)} %bitcast.41, s32[768]{0:T(1024)S(1)} %iota_add_fusion, f32[256]{0:T(256)S(1)} %bitcast.38, s32[256]{0:T(256)S(1)} %bitcast.35), kind=kOutput, calls=%fused_computation.1 | convolution fusion | flops 706609152 | bytes 5380096 | tf_op jit(solution)/shard_map/dot_general | solution.py:123
  40.2 1.2 %copy-done = f32[256,1792]{1,0:T(8,128)} copy-done((f32[256,1792]{1,0:T(8,128)}, f32[256,1792]{1,0:T(8,128)S(1)}, u32[]{:S(2)}) %copy-start) | copy-done | bytes 1835032
  41.7 3.0 %fusion.2 = f32[256,1792]{1,0:T(8,128)S(1)} fusion(bf16[768,3584]{1,0:T(8,128)(2,1)} %param.5, f32[256,768]{1,0:T(8,128)S(1)} %get-tuple-element.11, f32[256]{0:T(256)S(1)} %bitcast.42, s32[768]{0:T(1024)S(1)} %iota_add_fusion, f32[256]{0:T(256)S(1)} %bitcast.39, s32[256]{0:T(256)S(1)} %bitcast.36), kind=kOutput, calls=%fused_computation.3 | convolution fusion | flops 706609152 | bytes 5380096 | tf_op jit(solution)/shard_map/dot_general | solution.py:122
  47.5 5.6 %collective-permute-done.10 = bf16[2,32,1792]{2,1,0:T(8,128)(2,1)S(1)} collective-permute-done((bf16[2,32,1792]{2,1,0:T(8,128)(2,1)S(1)}, bf16[2,32,1792]{2,1,0:T(8,128)(2,1)S(1)}, u32[]{:S(2)}, u32[]{:S(2)}) %collective-permute-start.10) | collective-permute-done | bytes 229408 | tf_op jit(solution)/shard_map/ppermute | solution.py:13
  53.8 0.9 %collective-permute-done.7 = bf16[64,1792]{1,0:T(8,128)(2,1)S(1)} collective-permute-done((bf16[64,1792]{1,0:T(8,128)(2,1)S(1)}, bf16[64,1792]{1,0:T(8,128)(2,1)S(1)}, u32[]{:S(2)}, u32[]{:S(2)}) %collective-permute-start.7) | collective-permute-done | bytes 229408 | tf_op jit(solution)/shard_map/ppermute | solution.py:13
  55.5 2.4 %collective-permute-done.11 = bf16[32,1792]{1,0:T(8,128)(2,1)S(1)} collective-permute-done((bf16[32,1792]{1,0:T(8,128)(2,1)S(1)}, bf16[32,1792]{1,0:T(8,128)(2,1)S(1)}, u32[]{:S(2)}, u32[]{:S(2)}) %collective-permute-start.11) | collective-permute-done | bytes 114720 | tf_op jit(solution)/shard_map/ppermute | solution.py:13
  58.0 1.7 %collective-permute-done.8 = bf16[1,32,1792]{2,1,0:T(8,128)(2,1)S(1)} collective-permute-done((bf16[1,32,1792]{2,1,0:T(8,128)(2,1)S(1)}, bf16[1,32,1792]{2,1,0:T(8,128)(2,1)S(1)}, u32[]{:S(2)}, u32[]{:S(2)}) %collective-permute-start.8) | collective-permute-done | bytes 114720 | tf_op jit(solution)/shard_map/ppermute | solution.py:13
  59.8 0.8 collective-permute-start.12
  60.5 2.2 %collective-permute-start.14 = (bf16[8,3584]{1,0:T(8,128)(2,1)S(1)}, bf16[8,3584]{1,0:T(8,128)(2,1)S(1)}, u32[]{:S(2)}, u32[]{:S(2)}) collective-permute-start(bf16[8,3584]{1,0:T(8,128)(2,1)S(1)} %get-tuple-element.5), channel_id=1, source_target_pairs={{0,6},{1,7},{2,0},{3,1},{4,2},{5,3},{6,4},{7,5},{8,14},{9,15},{10,... | collective-permute-start | bytes 172040 | tf_op jit(solution)/shard_map/ppermute | solution.py:66
  62.7 3.4 %collective-permute-done.12 = bf16[8,3584]{1,0:T(8,128)(2,1)S(1)} collective-permute-done((bf16[8,3584]{1,0:T(8,128)(2,1)S(1)}, bf16[8,3584]{1,0:T(8,128)(2,1)S(1)}, u32[]{:S(2)}, u32[]{:S(2)}) %collective-permute-start.12) | collective-permute-done | bytes 57376 | tf_op jit(solution)/shard_map/ppermute | solution.py:66
  66.1 2.9 %collective-permute-done.13 = bf16[8,3584]{1,0:T(8,128)(2,1)S(1)} collective-permute-done((bf16[8,3584]{1,0:T(8,128)(2,1)S(1)}, bf16[8,3584]{1,0:T(8,128)(2,1)S(1)}, u32[]{:S(2)}, u32[]{:S(2)}) %collective-permute-start.13) | collective-permute-done | bytes 57376 | tf_op jit(solution)/shard_map/ppermute | solution.py:66
  69.7 3.3 %collective-permute-start.17 = (bf16[8,3584]{1,0:T(8,128)(2,1)S(1)}, bf16[8,3584]{1,0:T(8,128)(2,1)S(1)}, u32[]{:S(2)}, u32[]{:S(2)}) collective-permute-start(bf16[8,3584]{1,0:T(8,128)(2,1)S(1)} %get-tuple-element.3), channel_id=1, source_target_pairs={{0,6},{1,7},{2,0},{3,1},{4,2},{5,3},{6,4},{7,5},{8,14},{9,15},{10,... | collective-permute-start | bytes 172040 | tf_op jit(solution)/shard_map/ppermute | solution.py:66
  73.0 1.1 %collective-permute-done.15 = bf16[8,3584]{1,0:T(8,128)(2,1)S(1)} collective-permute-done((bf16[8,3584]{1,0:T(8,128)(2,1)S(1)}, bf16[8,3584]{1,0:T(8,128)(2,1)S(1)}, u32[]{:S(2)}, u32[]{:S(2)}) %collective-permute-start.15) | collective-permute-done | bytes 57376 | tf_op jit(solution)/shard_map/ppermute | solution.py:66
  74.1 1.0 %collective-permute-done.16 = bf16[8,3584]{1,0:T(8,128)(2,1)S(1)} collective-permute-done((bf16[8,3584]{1,0:T(8,128)(2,1)S(1)}, bf16[8,3584]{1,0:T(8,128)(2,1)S(1)}, u32[]{:S(2)}, u32[]{:S(2)}) %collective-permute-start.16) | collective-permute-done | bytes 57376 | tf_op jit(solution)/shard_map/ppermute | solution.py:66
  76.1 4.2 %convolution_convert_fusion = bf16[768,3584]{1,0:T(8,128)(2,1)} fusion(bf16[256,3584]{1,0:T(8,128)(2,1)S(1)} %constant_dynamic-update-slice_fusion, f32[256,768]{1,0:T(8,128)S(1)} %get-tuple-element.11, f32[256]{0:T(256)S(1)} %bitcast.43, s32[768]{0:T(1024)S(1)} %iota_add_fusion, f32[256]{0:T(256)S(1)} %bitcast.40, s32[256]{0:T(256)S(1)} %bitcast.37), kind=kOutput, calls=%fused_computation | convolution fusion | flops 1414004736 | bytes 8132608 | tf_op jit(solution)/shard_map/dot_general | solution.py:125
  80.4 1.1 %collective-permute-done.18 = bf16[32,3584]{1,0:T(8,128)(2,1)S(1)} collective-permute-done((bf16[32,3584]{1,0:T(8,128)(2,1)S(1)}, bf16[32,3584]{1,0:T(8,128)(2,1)S(1)}, u32[]{:S(2)}, u32[]{:S(2)}) %collective-permute-start.18) | collective-permute-done | bytes 229408 | tf_op jit(solution)/shard_map/ppermute | solution.py:13
  81.5 0.8 %maximum_select_fusion = bf16[64,3584]{1,0:T(8,128)(2,1)} fusion(bf16[32,3584]{1,0:T(8,128)(2,1)S(1)} %collective-permute-done.18, bf16[32,3584]{1,0:T(8,128)(2,1)S(1)} %constant_dynamic-update-slice_fusion.4, pred[]{:T(512)S(6)} %eq.37), kind=kLoop, calls=%fused_computation.20 | loop fusion | flops 2064384 | bytes 917505 | tf_op jit(solution)/shard_map/jit(_where)/select_n | solution.py:96
  (68 shorter events, 10.2 us)
Async XLA Ops:
  2.0 27.9 %collective-permute-start.1 = (f32[64,2]{0,1:T(2,128)S(1)}, f32[64,2]{0,1:T(2,128)S(1)}, u32[]{:S(2)}, u32[]{:S(2)}) collective-permute-start(f32[64,2]{0,1:T(2,128)S(1)} %pad_maximum_fusion.2), channel_id=1, source_target_pairs={{0,8},{8,0},{16,24},{24,16},{1,9},{9,1},{17,25},{25,17},{2,10},{10... | collective-permute-start | bytes 1544 | tf_op jit(solution)/shard_map/ppermute | solution.py:13
  2.5 4.1 %collective-permute-start = (f32[64,2]{0,1:T(2,128)S(1)}, f32[64,2]{0,1:T(2,128)S(1)}, u32[]{:S(2)}, u32[]{:S(2)}) collective-permute-start(f32[64,2]{0,1:T(2,128)S(1)} %pad_maximum_fusion.2), channel_id=1, source_target_pairs={{0,16},{8,24},{16,0},{24,8},{1,17},{9,25},{17,1},{25,9},{2,18},{10... | collective-permute-start | bytes 1544 | tf_op jit(solution)/shard_map/ppermute | solution.py:13
  5.1 12.8 %collective-permute-start.3 = (bf16[64,3584]{1,0:T(8,128)(2,1)}, bf16[64,3584]{1,0:T(8,128)(2,1)S(1)}, u32[]{:S(2)}, u32[]{:S(2)}) collective-permute-start(bf16[64,3584]{1,0:T(8,128)(2,1)} %param.4), channel_id=1, source_target_pairs={{0,16},{8,24},{16,0},{24,8},{1,17},{9,25},{17,1},{25,9},{2,18},{10... | collective-permute-start | bytes 1376264 | tf_op jit(solution)/shard_map/ppermute | solution.py:13
  5.2 12.7 %collective-permute-start.4 = (bf16[64,3584]{1,0:T(8,128)(2,1)}, bf16[64,3584]{1,0:T(8,128)(2,1)S(1)}, u32[]{:S(2)}, u32[]{:S(2)}) collective-permute-start(bf16[64,3584]{1,0:T(8,128)(2,1)} %param.4), channel_id=1, source_target_pairs={{0,8},{8,0},{16,24},{24,16},{1,9},{9,1},{17,25},{25,17},{2,10},{10... | collective-permute-start | bytes 1376264 | tf_op jit(solution)/shard_map/ppermute | solution.py:13
  6.6 23.2 %collective-permute-start.2 = (f32[64,2]{0,1:T(2,128)S(1)}, f32[64,2]{0,1:T(2,128)S(1)}, u32[]{:S(2)}, u32[]{:S(2)}) collective-permute-start(f32[64,2]{0,1:T(2,128)S(1)} %collective-permute-done), channel_id=1, source_target_pairs={{0,8},{8,0},{16,24},{24,16},{1,9},{9,1},{17,25},{25,17},{2,10},{10... | collective-permute-start | bytes 1544 | tf_op jit(solution)/shard_map/ppermute | solution.py:13
  17.9 1.8 %collective-permute-start.5 = (bf16[64,3584]{1,0:T(8,128)(2,1)S(1)}, bf16[64,3584]{1,0:T(8,128)(2,1)S(1)}, u32[]{:S(2)}, u32[]{:S(2)}) collective-permute-start(bf16[64,3584]{1,0:T(8,128)(2,1)S(1)} %collective-permute-done.3), channel_id=1, source_target_pairs={{0,8},{8,0},{16,24},{24,16},{1,9},{9,1},{17,25},{25,17},{2,10},{10... | collective-permute-start | bytes 1376264 | tf_op jit(solution)/shard_map/ppermute | solution.py:13
  24.9 12.1 %all-to-all-start = ((f32[32,1,256]{2,1,0:T(1,128)}), f32[32,1,256]{2,1,0:T(1,128)S(1)}, u32[]{:S(2)}, u32[]{:S(2)}) async-start(f32[32,1,256]{2,1,0:T(1,128)} %broadcast_in_dim.27), calls=%async_computation | async-start | bytes 65536 | tf_op jit(solution)/shard_map/all_to_all | solution.py:114
  40.2 1.2 %copy-start = (f32[256,1792]{1,0:T(8,128)}, f32[256,1792]{1,0:T(8,128)S(1)}, u32[]{:S(2)}) copy-start(f32[256,1792]{1,0:T(8,128)S(1)} %fusion) | copy-start | bytes 5505028
  41.5 3.7 %collective-permute-start.9 = (bf16[128,1792]{1,0:T(8,128)(2,1)S(1)}, bf16[128,1792]{1,0:T(8,128)(2,1)S(1)}, u32[]{:S(2)}, u32[]{:S(2)}) collective-permute-start(bf16[128,1792]{1,0:T(8,128)(2,1)S(1)} %slice.85), channel_id=1, source_target_pairs={{0,8},{8,0},{16,24},{24,16},{1,9},{9,1},{17,25},{25,17},{2,10},{10... | collective-permute-start | bytes 1376264 | tf_op jit(solution)/shard_map/ppermute | solution.py:13
  41.7 3.5 %copy-start.1 = (f32[256,1792]{1,0:T(8,128)S(1)}, f32[256,1792]{1,0:T(8,128)}, u32[]{:S(2)}) copy-start(f32[256,1792]{1,0:T(8,128)} %copy-done) | copy-start | bytes 5505028
  44.8 1.9 %collective-permute-start.6 = (bf16[128,1792]{1,0:T(8,128)(2,1)S(1)}, bf16[128,1792]{1,0:T(8,128)(2,1)S(1)}, u32[]{:S(2)}, u32[]{:S(2)}) collective-permute-start(bf16[128,1792]{1,0:T(8,128)(2,1)S(1)} %slice.86), channel_id=1, source_target_pairs={{0,8},{8,0},{16,24},{24,16},{1,9},{9,1},{17,25},{25,17},{2,10},{10... | collective-permute-start | bytes 1376264 | tf_op jit(solution)/shard_map/ppermute | solution.py:13
  45.4 7.7 %collective-permute-start.10 = (bf16[2,32,1792]{2,1,0:T(8,128)(2,1)S(1)}, bf16[2,32,1792]{2,1,0:T(8,128)(2,1)S(1)}, u32[]{:S(2)}, u32[]{:S(2)}) collective-permute-start(bf16[2,32,1792]{2,1,0:T(8,128)(2,1)S(1)} %dynamic-slice_convert_fusion), channel_id=1, source_target_pairs={{0,1},{1,0},{2,3},{3,2},{4,5},{5,4},{6,7},{7,6},{8,9},{9,8},{10,11... | collective-permute-start | bytes 688136 | tf_op jit(solution)/shard_map/ppermute | solution.py:13
  46.8 7.9 %collective-permute-start.7 = (bf16[64,1792]{1,0:T(8,128)(2,1)S(1)}, bf16[64,1792]{1,0:T(8,128)(2,1)S(1)}, u32[]{:S(2)}, u32[]{:S(2)}) collective-permute-start(bf16[64,1792]{1,0:T(8,128)(2,1)S(1)} %slice.87), channel_id=1, source_target_pairs={{0,16},{8,24},{16,0},{24,8},{1,17},{9,25},{17,1},{25,9},{2,18},{10... | collective-permute-start | bytes 688136 | tf_op jit(solution)/shard_map/ppermute | solution.py:13
  53.1 4.9 %collective-permute-start.11 = (bf16[32,1792]{1,0:T(8,128)(2,1)S(1)}, bf16[32,1792]{1,0:T(8,128)(2,1)S(1)}, u32[]{:S(2)}, u32[]{:S(2)}) collective-permute-start(bf16[32,1792]{1,0:T(8,128)(2,1)S(1)} %fusion.10), channel_id=1, source_target_pairs={{0,16},{8,24},{16,0},{24,8},{1,17},{9,25},{17,1},{25,9},{2,18},{10... | collective-permute-start | bytes 344072 | tf_op jit(solution)/shard_map/ppermute | solution.py:13
  54.8 4.9 %collective-permute-start.8 = (bf16[1,32,1792]{2,1,0:T(8,128)(2,1)S(1)}, bf16[1,32,1792]{2,1,0:T(8,128)(2,1)S(1)}, u32[]{:S(2)}, u32[]{:S(2)}) collective-permute-start(bf16[1,32,1792]{2,1,0:T(8,128)(2,1)S(1)} %fusion.9), channel_id=1, source_target_pairs={{0,1},{1,0},{2,3},{3,2},{4,5},{5,4},{6,7},{7,6},{8,9},{9,8},{10,11... | collective-permute-start | bytes 344072 | tf_op jit(solution)/shard_map/ppermute | solution.py:13
  59.8 6.3 %collective-permute-start.12 = (bf16[8,3584]{1,0:T(8,128)(2,1)S(1)}, bf16[8,3584]{1,0:T(8,128)(2,1)S(1)}, u32[]{:S(2)}, u32[]{:S(2)}) collective-permute-start(bf16[8,3584]{1,0:T(8,128)(2,1)S(1)} %get-tuple-element.4), channel_id=1, source_target_pairs={{0,4},{1,5},{2,6},{3,7},{4,0},{5,1},{6,2},{7,3},{8,12},{9,13},{10,... | collective-permute-start | bytes 172040 | tf_op jit(solution)/shard_map/ppermute | solution.py:66
  60.5 5.5 %collective-permute-start.14 = (bf16[8,3584]{1,0:T(8,128)(2,1)S(1)}, bf16[8,3584]{1,0:T(8,128)(2,1)S(1)}, u32[]{:S(2)}, u32[]{:S(2)}) collective-permute-start(bf16[8,3584]{1,0:T(8,128)(2,1)S(1)} %get-tuple-element.5), channel_id=1, source_target_pairs={{0,6},{1,7},{2,0},{3,1},{4,2},{5,3},{6,4},{7,5},{8,14},{9,15},{10,... | collective-permute-start | bytes 172040 | tf_op jit(solution)/shard_map/ppermute | solution.py:66
  62.7 6.2 %collective-permute-start.13 = (bf16[8,3584]{1,0:T(8,128)(2,1)S(1)}, bf16[8,3584]{1,0:T(8,128)(2,1)S(1)}, u32[]{:S(2)}, u32[]{:S(2)}) collective-permute-start(bf16[8,3584]{1,0:T(8,128)(2,1)S(1)} %get-tuple-element.6), channel_id=1, source_target_pairs={{0,2},{1,3},{2,4},{3,5},{4,6},{5,7},{6,0},{7,1},{8,10},{9,11},{10,... | collective-permute-start | bytes 172040 | tf_op jit(solution)/shard_map/ppermute | solution.py:66
  69.0 5.1 %collective-permute-start.15 = (bf16[8,3584]{1,0:T(8,128)(2,1)S(1)}, bf16[8,3584]{1,0:T(8,128)(2,1)S(1)}, u32[]{:S(2)}, u32[]{:S(2)}) collective-permute-start(bf16[8,3584]{1,0:T(8,128)(2,1)S(1)} %get-tuple-element.3), channel_id=1, source_target_pairs={{0,4},{1,5},{2,6},{3,7},{4,0},{5,1},{6,2},{7,3},{8,12},{9,13},{10,... | collective-permute-start | bytes 172040 | tf_op jit(solution)/shard_map/ppermute | solution.py:66
  69.1 6.0 %collective-permute-start.16 = (bf16[8,3584]{1,0:T(8,128)(2,1)S(1)}, bf16[8,3584]{1,0:T(8,128)(2,1)S(1)}, u32[]{:S(2)}, u32[]{:S(2)}) collective-permute-start(bf16[8,3584]{1,0:T(8,128)(2,1)S(1)} %get-tuple-element.3), channel_id=1, source_target_pairs={{0,2},{1,3},{2,4},{3,5},{4,6},{5,7},{6,0},{7,1},{8,10},{9,11},{10,... | collective-permute-start | bytes 172040 | tf_op jit(solution)/shard_map/ppermute | solution.py:66
  69.7 5.7 %collective-permute-start.17 = (bf16[8,3584]{1,0:T(8,128)(2,1)S(1)}, bf16[8,3584]{1,0:T(8,128)(2,1)S(1)}, u32[]{:S(2)}, u32[]{:S(2)}) collective-permute-start(bf16[8,3584]{1,0:T(8,128)(2,1)S(1)} %get-tuple-element.3), channel_id=1, source_target_pairs={{0,6},{1,7},{2,0},{3,1},{4,2},{5,3},{6,4},{7,5},{8,14},{9,15},{10,... | collective-permute-start | bytes 172040 | tf_op jit(solution)/shard_map/ppermute | solution.py:66
  75.4 6.1 %collective-permute-start.18 = (bf16[32,3584]{1,0:T(8,128)(2,1)S(1)}, bf16[32,3584]{1,0:T(8,128)(2,1)S(1)}, u32[]{:S(2)}, u32[]{:S(2)}) collective-permute-start(bf16[32,3584]{1,0:T(8,128)(2,1)S(1)} %constant_dynamic-update-slice_fusion.4), channel_id=1, source_target_pairs={{0,1},{1,0},{2,3},{3,2},{4,5},{5,4},{6,7},{7,6},{8,9},{9,8},{10,11... | collective-permute-start | bytes 688136 | tf_op jit(solution)/shard_map/ppermute | solution.py:13

commit v3 on v2

--- a/solution.py
+++ b/solution.py
@@ -61,15 +61,6 @@
     return (take(x, place, half, 1).astype(f32) + other.astype(f32)).reshape(blocks * half, -1)
 
 
-def shift_pairs(x, k):
-    size = lax.axis_size("vocab")
-    return lax.ppermute(x, "vocab", [(i, (i + 2 * k) % size) for i in range(size)])
-
-
-def hops(count):
-    return sorted(range(1, count), key=lambda k: -min(k, count - k))
-
-
 def reduce_hidden(left, right):
     near, *far = axis_bits("dp")
     left, right = halve(left, near), halve(right, near)
@@ -80,17 +71,9 @@
         right = halve(right, bit)
     left = halve_vocab(left, 1)
     part = jnp.concatenate([left, right], axis=1)
-    count = lax.axis_size("vocab") // 2
-    place = lax.axis_index("vocab") // 2
-    rows = part.shape[0] // count
-    total = take(part, place, rows)
-    sent = part.astype(bf16)
-    for k in hops(count):
-        total = total + shift_pairs(take(sent, (place + k) % count, rows), k).astype(f32)
-    total = total.astype(bf16)
-    out = jnp.zeros(part.shape, bf16)
-    for k, piece in [(0, total)] + [(k, shift_pairs(total, k)) for k in hops(count)]:
-        out = lax.dynamic_update_slice_in_dim(out, piece, ((place - k) % count) * rows, 0)
+    for bit in axis_bits("vocab")[1:]:
+        part = part + exchange(part.astype(bf16), "vocab", bit).astype(f32)
+    out = part.astype(bf16)
     other = exchange(out, "vocab", 1)
     low = lax.axis_index("vocab") % 2 == 0
     return jnp.where(low, jnp.concatenate([out, other], 0), jnp.concatenate([other, out], 0))

time: 82.6 us -> 85.1 us (1.030)
  waiting for transfers between devices: 41 us -> 48.2 us
  starting transfers between devices: 19.5 us -> 14 us
  other arithmetic: 2.72 us -> 3.72 us
    ppermute x13 -> x15, waiting for transfers between devices: 25.3 us -> 41.1 us  [exchange(): lax.ppermute(x, axis, [(i, i ^ bit) for i in range(lax.axis_size(axis))])]
    ppermute x6 -> x0, waiting for transfers between devices: 8.57 us -> none  [shift_pairs(): lax.ppermute(x, 'vocab', [(i, (i + 2 * k) % size) for i in range(size)])]
    ppermute x6 -> x0, starting transfers between devices: 6.87 us -> none  [shift_pairs(): lax.ppermute(x, 'vocab', [(i, (i + 2 * k) % size) for i in range(size)])]
    ppermute x13 -> x15, starting transfers between devices: 7.75 us -> 9.09 us  [exchange(): lax.ppermute(x, axis, [(i, i ^ bit) for i in range(lax.axis_size(axis))])]
    convert_element_type x1 -> x3, other arithmetic: 0.03 us -> 1.08 us  [the longest x1 1.01 us: reduce_hidden(): out = part.astype(bf16)]
  transfers between devices with their start and end apart: 20 -> 16, of which waited for: 15 -> 12; matrix products, arithmetic and copies ran while one was open for 17% -> 17% of each run, Pallas kernels for 0% -> 0%
where the time goes in v3:
time: 85.1 us; the launch traced here: 84.8 us
  waiting for transfers between devices  48.2 us (57%)
  matrix products  14.5 us (17%)
  starting transfers between devices  14 us (16%)
  other arithmetic  3.72 us (4%)
  local copies, waits for them, and re-layouts  3.61 us (4%)
    ppermute x15, waiting for transfers between devices, exchange(): lax.ppermute(x, axis, [(i, i ^ bit) for i in range(lax.axis_size(axis))])  41.1 us
    ppermute x15, starting transfers between devices, exchange(): lax.ppermute(x, axis, [(i, i ^ bit) for i in range(lax.axis_size(axis))])  9.09 us
    all_to_all x1, waiting for transfers between devices, body(): totals = lax.all_to_all(spread, both, 0, 0)  7.09 us
    all_to_all x1, starting transfers between devices, body(): totals = lax.all_to_all(spread, both, 0, 0)  4.89 us
    dot_general x1, matrix products, body(): lax.dot_general(group_hidden, embedding, (((1,), (1,)), ((), ())), prefer...  4.34 us
    dot_general x1, matrix products, body(): lax.dot_general(scores_grad, group_hidden, (((0,), (0,)), ((), ())), pref...  4.25 us
    dot_general x1, matrix products, body(): left = jnp.dot(scores_grad, embedding[:, :cut], preferred_element_type=f32)  3.01 us
    dot_general x1, matrix products, body(): right = jnp.dot(scores_grad, embedding[:, cut:], preferred_element_type=f32)  2.89 us
  transfers between devices with their start and end apart: 16, of which 12 were waited for; matrix products, arithmetic and copies ran while one was open for 17% of the time, Pallas kernels for 0%

profile of v3, /device:TPU:0, one launch (start us, length us, event | category | flops | bytes accessed | tf_op | source)
XLA Modules:
  0.0 84.8 jit_solution(6363270706195285566)
XLA Ops:
  2.5 2.6 %collective-permute-start = (f32[64,2]{0,1:T(2,128)S(1)}, f32[64,2]{0,1:T(2,128)S(1)}, u32[]{:S(2)}, u32[]{:S(2)}) collective-permute-start(f32[64,2]{0,1:T(2,128)S(1)} %pad_maximum_fusion.2), channel_id=1, source_target_pairs={{0,16},{8,24},{16,0},{24,8},{1,17},{9,25},{17,1},{25,9},{2,18},{10... | collective-permute-start | bytes 1544 | tf_op jit(solution)/shard_map/ppermute | solution.py:13
  5.3 1.0 %constant_dynamic-update-slice_fusion.3 = bf16[256,3584]{1,0:T(8,128)(2,1)S(1)} fusion(bf16[64,3584]{1,0:T(8,128)(2,1)} %param.4), kind=kLoop, calls=%fused_computation.35 | loop fusion | bytes 917504
  6.8 11.0 %collective-permute-done.3 = bf16[64,3584]{1,0:T(8,128)(2,1)S(1)} collective-permute-done((bf16[64,3584]{1,0:T(8,128)(2,1)}, bf16[64,3584]{1,0:T(8,128)(2,1)S(1)}, u32[]{:S(2)}, u32[]{:S(2)}) %collective-permute-start.3) | collective-permute-done | bytes 458784 | tf_op jit(solution)/shard_map/ppermute | solution.py:13
  18.0 1.7 %collective-permute-done.5 = bf16[64,3584]{1,0:T(8,128)(2,1)S(1)} collective-permute-done((bf16[64,3584]{1,0:T(8,128)(2,1)S(1)}, bf16[64,3584]{1,0:T(8,128)(2,1)S(1)}, u32[]{:S(2)}, u32[]{:S(2)}) %collective-permute-start.5) | collective-permute-done | bytes 458784 | tf_op jit(solution)/shard_map/ppermute | solution.py:13
  19.7 4.3 %fusion.5 = (f32[256]{0:T(256)S(1)}, f32[256,768]{1,0:T(8,128)S(1)}) fusion(bf16[256,3584]{1,0:T(8,128)(2,1)S(1)} %constant_dynamic-update-slice_fusion, bf16[768,3584]{1,0:T(8,128)(2,1)} %param.5), kind=kOutput, calls=%fused_computation.13 | convolution fusion | flops 1410072320 | bytes 8127488 | tf_op jit(solution)/shard_map/dot_general | solution.py:90
  24.9 4.9 %all-to-all-start = ((f32[32,1,256]{2,1,0:T(1,128)}), f32[32,1,256]{2,1,0:T(1,128)S(1)}, u32[]{:S(2)}, u32[]{:S(2)}) async-start(f32[32,1,256]{2,1,0:T(1,128)} %broadcast_in_dim.23), calls=%async_computation | async-start | bytes 65536 | tf_op jit(solution)/shard_map/all_to_all | solution.py:97
  29.9 7.1 %all-to-all-done = f32[32,1,256]{2,1,0:T(1,128)S(1)} async-done(((f32[32,1,256]{2,1,0:T(1,128)}), f32[32,1,256]{2,1,0:T(1,128)S(1)}, u32[]{:S(2)}, u32[]{:S(2)}) %all-to-all-start) | async-done | bytes 32800 | tf_op jit(solution)/shard_map/all_to_all | solution.py:97
  37.3 2.9 %fusion = f32[256,1792]{1,0:T(8,128)S(1)} fusion(bf16[768,3584]{1,0:T(8,128)(2,1)} %param.5, f32[256,768]{1,0:T(8,128)S(1)} %get-tuple-element.6, f32[256]{0:T(256)S(1)} %bitcast.41, s32[768]{0:T(1024)S(1)} %iota_add_fusion, f32[256]{0:T(256)S(1)} %bitcast.38, s32[256]{0:T(256)S(1)} %bitcast.35), kind=kOutput, calls=%fused_computation.1 | convolution fusion | flops 706609152 | bytes 5380096 | tf_op jit(solution)/shard_map/dot_general | solution.py:106
  40.2 1.2 %copy-done = f32[256,1792]{1,0:T(8,128)} copy-done((f32[256,1792]{1,0:T(8,128)}, f32[256,1792]{1,0:T(8,128)S(1)}, u32[]{:S(2)}) %copy-start) | copy-done | bytes 1835032
  41.7 3.0 %fusion.2 = f32[256,1792]{1,0:T(8,128)S(1)} fusion(bf16[768,3584]{1,0:T(8,128)(2,1)} %param.5, f32[256,768]{1,0:T(8,128)S(1)} %get-tuple-element.6, f32[256]{0:T(256)S(1)} %bitcast.42, s32[768]{0:T(1024)S(1)} %iota_add_fusion, f32[256]{0:T(256)S(1)} %bitcast.39, s32[256]{0:T(256)S(1)} %bitcast.36), kind=kOutput, calls=%fused_computation.3 | convolution fusion | flops 706609152 | bytes 5380096 | tf_op jit(solution)/shard_map/dot_general | solution.py:105
  45.4 0.7 collective-permute-start.10
  47.5 5.6 %collective-permute-done.10 = bf16[2,32,1792]{2,1,0:T(8,128)(2,1)S(1)} collective-permute-done((bf16[2,32,1792]{2,1,0:T(8,128)(2,1)S(1)}, bf16[2,32,1792]{2,1,0:T(8,128)(2,1)S(1)}, u32[]{:S(2)}, u32[]{:S(2)}) %collective-permute-start.10) | collective-permute-done | bytes 229408 | tf_op jit(solution)/shard_map/ppermute | solution.py:13
  53.7 1.0 %collective-permute-done.7 = bf16[64,1792]{1,0:T(8,128)(2,1)S(1)} collective-permute-done((bf16[64,1792]{1,0:T(8,128)(2,1)S(1)}, bf16[64,1792]{1,0:T(8,128)(2,1)S(1)}, u32[]{:S(2)}, u32[]{:S(2)}) %collective-permute-start.7) | collective-permute-done | bytes 229408 | tf_op jit(solution)/shard_map/ppermute | solution.py:13
  54.8 0.7 collective-permute-start.8
  55.6 2.4 %collective-permute-done.11 = bf16[32,1792]{1,0:T(8,128)(2,1)S(1)} collective-permute-done((bf16[32,1792]{1,0:T(8,128)(2,1)S(1)}, bf16[32,1792]{1,0:T(8,128)(2,1)S(1)}, u32[]{:S(2)}, u32[]{:S(2)}) %collective-permute-start.11) | collective-permute-done | bytes 114720 | tf_op jit(solution)/shard_map/ppermute | solution.py:13
  58.0 1.7 %collective-permute-done.8 = bf16[1,32,1792]{2,1,0:T(8,128)(2,1)S(1)} collective-permute-done((bf16[1,32,1792]{2,1,0:T(8,128)(2,1)S(1)}, bf16[1,32,1792]{2,1,0:T(8,128)(2,1)S(1)}, u32[]{:S(2)}, u32[]{:S(2)}) %collective-permute-start.8) | collective-permute-done | bytes 114720 | tf_op jit(solution)/shard_map/ppermute | solution.py:13
  60.3 5.5 %collective-permute-done.12 = bf16[32,3584]{1,0:T(8,128)(2,1)S(1)} collective-permute-done((bf16[32,3584]{1,0:T(8,128)(2,1)S(1)}, bf16[32,3584]{1,0:T(8,128)(2,1)S(1)}, u32[]{:S(2)}, u32[]{:S(2)}) %collective-permute-start.12) | collective-permute-done | bytes 229408 | tf_op jit(solution)/shard_map/ppermute | solution.py:13
  65.9 0.8 collective-permute-start.13
  66.6 9.9 %collective-permute-done.13 = bf16[32,3584]{1,0:T(8,128)(2,1)} collective-permute-done((bf16[32,3584]{1,0:T(8,128)(2,1)S(1)}, bf16[32,3584]{1,0:T(8,128)(2,1)}, u32[]{:S(2)}, u32[]{:S(2)}) %collective-permute-start.13) | collective-permute-done | bytes 229408 | tf_op jit(solution)/shard_map/ppermute | solution.py:13
  76.6 1.0 %add_convert_fusion = bf16[32,3584]{1,0:T(8,128)(2,1)S(1)} fusion(bf16[32,3584]{1,0:T(8,128)(2,1)} %collective-permute-done.13, bf16[32,3584]{1,0:T(8,128)(2,1)S(1)} %collective-permute-done.12, f32[32,1792]{1,0:T(8,128)S(1)} %fusion.8, f32[32,1792]{1,0:T(8,128)S(1)} %fusion.9), kind=kLoop, calls=%fused_computation.18 | loop fusion | flops 688128 | bytes 1146880 | tf_op jit(solution)/shard_map/convert_element_type | solution.py:76
  77.6 0.8 collective-permute-start.14
  78.4 4.2 %convolution_convert_fusion = bf16[768,3584]{1,0:T(8,128)(2,1)} fusion(bf16[256,3584]{1,0:T(8,128)(2,1)S(1)} %constant_dynamic-update-slice_fusion, f32[256,768]{1,0:T(8,128)S(1)} %get-tuple-element.6, f32[256]{0:T(256)S(1)} %bitcast.43, s32[768]{0:T(1024)S(1)} %iota_add_fusion, f32[256]{0:T(256)S(1)} %bitcast.40, s32[256]{0:T(256)S(1)} %bitcast.37), kind=kOutput, calls=%fused_computation | convolution fusion | flops 1414004736 | bytes 8132608 | tf_op jit(solution)/shard_map/dot_general | solution.py:108
  82.6 1.3 %collective-permute-done.14 = bf16[32,3584]{1,0:T(8,128)(2,1)S(1)} collective-permute-done((bf16[32,3584]{1,0:T(8,128)(2,1)S(1)}, bf16[32,3584]{1,0:T(8,128)(2,1)S(1)}, u32[]{:S(2)}, u32[]{:S(2)}) %collective-permute-start.14) | collective-permute-done | bytes 229408 | tf_op jit(solution)/shard_map/ppermute | solution.py:13
  84.0 0.8 maximum_select_fusion
  (56 shorter events, 7.6 us)
Async XLA Ops:
  2.0 27.9 %collective-permute-start.1 = (f32[64,2]{0,1:T(2,128)S(1)}, f32[64,2]{0,1:T(2,128)S(1)}, u32[]{:S(2)}, u32[]{:S(2)}) collective-permute-start(f32[64,2]{0,1:T(2,128)S(1)} %pad_maximum_fusion.2), channel_id=1, source_target_pairs={{0,8},{8,0},{16,24},{24,16},{1,9},{9,1},{17,25},{25,17},{2,10},{10... | collective-permute-start | bytes 1544 | tf_op jit(solution)/shard_map/ppermute | solution.py:13
  2.5 4.1 %collective-permute-start = (f32[64,2]{0,1:T(2,128)S(1)}, f32[64,2]{0,1:T(2,128)S(1)}, u32[]{:S(2)}, u32[]{:S(2)}) collective-permute-start(f32[64,2]{0,1:T(2,128)S(1)} %pad_maximum_fusion.2), channel_id=1, source_target_pairs={{0,16},{8,24},{16,0},{24,8},{1,17},{9,25},{17,1},{25,9},{2,18},{10... | collective-permute-start | bytes 1544 | tf_op jit(solution)/shard_map/ppermute | solution.py:13
  5.1 12.8 %collective-permute-start.3 = (bf16[64,3584]{1,0:T(8,128)(2,1)}, bf16[64,3584]{1,0:T(8,128)(2,1)S(1)}, u32[]{:S(2)}, u32[]{:S(2)}) collective-permute-start(bf16[64,3584]{1,0:T(8,128)(2,1)} %param.4), channel_id=1, source_target_pairs={{0,16},{8,24},{16,0},{24,8},{1,17},{9,25},{17,1},{25,9},{2,18},{10... | collective-permute-start | bytes 1376264 | tf_op jit(solution)/shard_map/ppermute | solution.py:13
  5.2 12.7 %collective-permute-start.4 = (bf16[64,3584]{1,0:T(8,128)(2,1)}, bf16[64,3584]{1,0:T(8,128)(2,1)S(1)}, u32[]{:S(2)}, u32[]{:S(2)}) collective-permute-start(bf16[64,3584]{1,0:T(8,128)(2,1)} %param.4), channel_id=1, source_target_pairs={{0,8},{8,0},{16,24},{24,16},{1,9},{9,1},{17,25},{25,17},{2,10},{10... | collective-permute-start | bytes 1376264 | tf_op jit(solution)/shard_map/ppermute | solution.py:13
  6.6 23.2 %collective-permute-start.2 = (f32[64,2]{0,1:T(2,128)S(1)}, f32[64,2]{0,1:T(2,128)S(1)}, u32[]{:S(2)}, u32[]{:S(2)}) collective-permute-start(f32[64,2]{0,1:T(2,128)S(1)} %collective-permute-done), channel_id=1, source_target_pairs={{0,8},{8,0},{16,24},{24,16},{1,9},{9,1},{17,25},{25,17},{2,10},{10... | collective-permute-start | bytes 1544 | tf_op jit(solution)/shard_map/ppermute | solution.py:13
  17.9 1.8 %collective-permute-start.5 = (bf16[64,3584]{1,0:T(8,128)(2,1)S(1)}, bf16[64,3584]{1,0:T(8,128)(2,1)S(1)}, u32[]{:S(2)}, u32[]{:S(2)}) collective-permute-start(bf16[64,3584]{1,0:T(8,128)(2,1)S(1)} %collective-permute-done.3), channel_id=1, source_target_pairs={{0,8},{8,0},{16,24},{24,16},{1,9},{9,1},{17,25},{25,17},{2,10},{10... | collective-permute-start | bytes 1376264 | tf_op jit(solution)/shard_map/ppermute | solution.py:13
  24.9 12.1 %all-to-all-start = ((f32[32,1,256]{2,1,0:T(1,128)}), f32[32,1,256]{2,1,0:T(1,128)S(1)}, u32[]{:S(2)}, u32[]{:S(2)}) async-start(f32[32,1,256]{2,1,0:T(1,128)} %broadcast_in_dim.23), calls=%async_computation | async-start | bytes 65536 | tf_op jit(solution)/shard_map/all_to_all | solution.py:97
  40.2 1.2 %copy-start = (f32[256,1792]{1,0:T(8,128)}, f32[256,1792]{1,0:T(8,128)S(1)}, u32[]{:S(2)}) copy-start(f32[256,1792]{1,0:T(8,128)S(1)} %fusion) | copy-start | bytes 5505028
  41.5 3.7 %collective-permute-start.9 = (bf16[128,1792]{1,0:T(8,128)(2,1)S(1)}, bf16[128,1792]{1,0:T(8,128)(2,1)S(1)}, u32[]{:S(2)}, u32[]{:S(2)}) collective-permute-start(bf16[128,1792]{1,0:T(8,128)(2,1)S(1)} %slice.85), channel_id=1, source_target_pairs={{0,8},{8,0},{16,24},{24,16},{1,9},{9,1},{17,25},{25,17},{2,10},{10... | collective-permute-start | bytes 1376264 | tf_op jit(solution)/shard_map/ppermute | solution.py:13
  41.7 3.5 %copy-start.1 = (f32[256,1792]{1,0:T(8,128)S(1)}, f32[256,1792]{1,0:T(8,128)}, u32[]{:S(2)}) copy-start(f32[256,1792]{1,0:T(8,128)} %copy-done) | copy-start | bytes 5505028
  44.8 1.9 %collective-permute-start.6 = (bf16[128,1792]{1,0:T(8,128)(2,1)S(1)}, bf16[128,1792]{1,0:T(8,128)(2,1)S(1)}, u32[]{:S(2)}, u32[]{:S(2)}) collective-permute-start(bf16[128,1792]{1,0:T(8,128)(2,1)S(1)} %slice.86), channel_id=1, source_target_pairs={{0,8},{8,0},{16,24},{24,16},{1,9},{9,1},{17,25},{25,17},{2,10},{10... | collective-permute-start | bytes 1376264 | tf_op jit(solution)/shard_map/ppermute | solution.py:13
  45.4 7.7 %collective-permute-start.10 = (bf16[2,32,1792]{2,1,0:T(8,128)(2,1)S(1)}, bf16[2,32,1792]{2,1,0:T(8,128)(2,1)S(1)}, u32[]{:S(2)}, u32[]{:S(2)}) collective-permute-start(bf16[2,32,1792]{2,1,0:T(8,128)(2,1)S(1)} %dynamic-slice_convert_fusion), channel_id=1, source_target_pairs={{0,1},{1,0},{2,3},{3,2},{4,5},{5,4},{6,7},{7,6},{8,9},{9,8},{10,11... | collective-permute-start | bytes 688136 | tf_op jit(solution)/shard_map/ppermute | solution.py:13
  46.8 7.9 %collective-permute-start.7 = (bf16[64,1792]{1,0:T(8,128)(2,1)S(1)}, bf16[64,1792]{1,0:T(8,128)(2,1)S(1)}, u32[]{:S(2)}, u32[]{:S(2)}) collective-permute-start(bf16[64,1792]{1,0:T(8,128)(2,1)S(1)} %slice.87), channel_id=1, source_target_pairs={{0,16},{8,24},{16,0},{24,8},{1,17},{9,25},{17,1},{25,9},{2,18},{10... | collective-permute-start | bytes 688136 | tf_op jit(solution)/shard_map/ppermute | solution.py:13
  53.1 4.9 %collective-permute-start.11 = (bf16[32,1792]{1,0:T(8,128)(2,1)S(1)}, bf16[32,1792]{1,0:T(8,128)(2,1)S(1)}, u32[]{:S(2)}, u32[]{:S(2)}) collective-permute-start(bf16[32,1792]{1,0:T(8,128)(2,1)S(1)} %fusion.11), channel_id=1, source_target_pairs={{0,16},{8,24},{16,0},{24,8},{1,17},{9,25},{17,1},{25,9},{2,18},{10... | collective-permute-start | bytes 344072 | tf_op jit(solution)/shard_map/ppermute | solution.py:13
  54.8 4.9 %collective-permute-start.8 = (bf16[1,32,1792]{2,1,0:T(8,128)(2,1)S(1)}, bf16[1,32,1792]{2,1,0:T(8,128)(2,1)S(1)}, u32[]{:S(2)}, u32[]{:S(2)}) collective-permute-start(bf16[1,32,1792]{2,1,0:T(8,128)(2,1)S(1)} %fusion.10), channel_id=1, source_target_pairs={{0,1},{1,0},{2,3},{3,2},{4,5},{5,4},{6,7},{7,6},{8,9},{9,8},{10,11... | collective-permute-start | bytes 344072 | tf_op jit(solution)/shard_map/ppermute | solution.py:13
  59.7 6.1 %collective-permute-start.12 = (bf16[32,3584]{1,0:T(8,128)(2,1)S(1)}, bf16[32,3584]{1,0:T(8,128)(2,1)S(1)}, u32[]{:S(2)}, u32[]{:S(2)}) collective-permute-start(bf16[32,3584]{1,0:T(8,128)(2,1)S(1)} %fusion.6), channel_id=1, source_target_pairs={{0,2},{1,3},{2,0},{3,1},{4,6},{5,7},{6,4},{7,5},{8,10},{9,11},{10,... | collective-permute-start | bytes 688136 | tf_op jit(solution)/shard_map/ppermute | solution.py:13
  65.9 10.7 %collective-permute-start.13 = (bf16[32,3584]{1,0:T(8,128)(2,1)S(1)}, bf16[32,3584]{1,0:T(8,128)(2,1)}, u32[]{:S(2)}, u32[]{:S(2)}) collective-permute-start(bf16[32,3584]{1,0:T(8,128)(2,1)S(1)} %fusion.7), channel_id=1, source_target_pairs={{0,4},{1,5},{2,6},{3,7},{4,0},{5,1},{6,2},{7,3},{8,12},{9,13},{10,... | collective-permute-start | bytes 688136 | tf_op jit(solution)/shard_map/ppermute | solution.py:13
  77.6 6.4 %collective-permute-start.14 = (bf16[32,3584]{1,0:T(8,128)(2,1)S(1)}, bf16[32,3584]{1,0:T(8,128)(2,1)S(1)}, u32[]{:S(2)}, u32[]{:S(2)}) collective-permute-start(bf16[32,3584]{1,0:T(8,128)(2,1)S(1)} %add_convert_fusion), channel_id=1, source_target_pairs={{0,1},{1,0},{2,3},{3,2},{4,5},{5,4},{6,7},{7,6},{8,9},{9,8},{10,11... | collective-permute-start | bytes 688136 | tf_op jit(solution)/shard_map/ppermute | solution.py:13
